TPU v7x, 32 devices: a whole 2x2x4 slice. The times are simulated.
32 devices in a mesh: cp: 16 (over z, y, x), hd: 2 (over core).
Axes of the slice: x: 2, y: 2, z: 4, core: 2. Of those that a mesh axis runs over, the one named last changes fastest.
Arguments:
- queries: bfloat16 [3072, 4096], P('cp', 'hd'), may hold values from -48 to 48
- keys: bfloat16 [3072, 1024], P('cp', 'hd'), may hold values from -48 to 48
- values: bfloat16 [3072, 1024], P('cp', 'hd'), may hold values from -6 to 6
- span_table: int32 [32], replicated, may hold values from 0 to 31, as said below
- doc_ids: int32 [3072], replicated, may hold values from 0 to 7, never falling along the last dimension, each value on 1 to 768 neighbouring positions
- out_weight: bfloat16 [4096, 4096], P('hd'), may hold values from -0.09375 to 0.09375
Outputs:
- mixed: bfloat16 [3072, 4096], P(('cp', 'hd'))
Inputs may be any that keep to these rules, and one draw needn't show every extreme that they name: `span_table`: slots 2 j and 2 j + 1 hold two spans c and 31 - c, and every span is held once.
All inputs are finite; a program needn't handle non-finite values.
Results may differ from a plain program's by a relative error of at most 0.0095.
Values may be sent and summed in bfloat16 or wider, within the bound.
A program may use at most 128 MiB of HBM per device.

v0:
```python
import functools
import math

import jax
import jax.numpy as jnp
from jax import lax
from jax.experimental import pallas as pl
from jax.experimental.pallas import tpu as pltpu
from jax.sharding import PartitionSpec as P

HEAD_WIDTH = 128
DOCS = 8
LANES = 256
NEG = -1e30
MESH = pl.DeviceIdType.MESH


def kernel(
    line, q_ref, span_ref, doc_ref, k_hbm, v_hbm, w_hbm, out_ref,
    kv, w_vmem, q_t, acc, best, total, fades, held, bias, low, high, attn, outgoing, incoming, kept,
    load_sem, w_sem, send0, send_z, send_xy, recv, out_send, out_recv,
):
    rows = q_ref.shape[0]
    span_len = rows // 2
    kv_heads = k_hbm.shape[1] // HEAD_WIDTH
    group = q_ref.shape[1] // HEAD_WIDTH // kv_heads
    tiles = group * rows // LANES
    whole = rows // 3
    side = (rows - whole) // 2
    me = lax.axis_index("cp")
    hd = lax.axis_index("hd")
    z = me // 4
    y = (me // 2) % 2
    x = me % 2

    def slot(zz, fx, fy):
        xx = 1 - x if fx else x
        yy = 1 - y if fy else y
        return zz * 4 + yy * 2 + xx

    piece_rows = {
        "A": (0, side, 0), "B": (side, side, 1), "C": (2 * side, whole, 2),
        "C0": (2 * side, whole // 2, 2), "C1": (2 * side + whole // 2, whole // 2, 3),
    }

    def part(src, piece):
        start, size, _ = piece_rows[piece]
        return kv.at[src, :, pl.ds(start, size), :]

    def copy_of(src, piece, target, sem):
        return pltpu.make_async_remote_copy(
            src_ref=part(src, piece), dst_ref=part(src, piece), send_sem=sem,
            recv_sem=recv.at[src, piece_rows[piece][2]],
            device_id={"cp": target}, device_id_type=MESH,
        )

    def arrived(src, piece):
        copy_of(src, piece, slot(z, True, False), send0.at[0]).wait_recv()

    to_x, to_y = slot(z, True, False), slot(z, False, True)
    up, down = me + 4, me - 4
    has_up, has_down = z < line - 1, z > 0

    loads = [
        pltpu.make_async_copy(k_hbm, kv.at[me, 0], load_sem.at[0]),
        pltpu.make_async_copy(v_hbm, kv.at[me, 1], load_sem.at[1]),
    ]
    w_load = pltpu.make_async_copy(w_hbm, w_vmem, w_sem)
    for load in loads:
        load.start()
    barrier = pltpu.get_barrier_semaphore()
    for target in (to_x, to_y):
        pl.semaphore_signal(barrier, inc=1, device_id={"cp": target}, device_id_type=MESH)
    pl.semaphore_signal(barrier, inc=1, device_id={"hd": 1 - hd}, device_id_type=MESH)

    @pl.when(has_up)
    def _():
        pl.semaphore_signal(barrier, inc=1, device_id={"cp": up}, device_id_type=MESH)

    @pl.when(has_down)
    def _():
        pl.semaphore_signal(barrier, inc=1, device_id={"cp": down}, device_id_type=MESH)

    pl.semaphore_wait(barrier, 3 + has_up.astype(jnp.int32) + has_down.astype(jnp.int32))
    for load in loads:
        load.wait()

    own, xn, yn, dg = (False, False), (True, False), (False, True), (True, True)
    first_x = [(own, "A"), (own, "C"), (own, "B")]
    first_y = [(own, "B"), (own, "C"), (own, "A")]
    first_z = [(own, "C"), (own, "A"), (own, "B")]
    later_z = [(xn, "A"), (yn, "B")]

    def first_stage(act, xs, ys, zs, nx, ny, nz):
        for i in range(max(len(xs), len(ys))):
            if i < len(xs):
                act(copy_of(slot(z, *xs[i][0]), xs[i][1], to_x, send0.at[nx + i]))
            if i < len(ys):
                act(copy_of(slot(z, *ys[i][0]), ys[i][1], to_y, send0.at[5 + ny + i]))

        @pl.when(has_up)
        def _():
            for i, (flips, piece) in enumerate(zs):
                act(copy_of(slot(z, *flips), piece, up, send0.at[10 + nz + i]))

        @pl.when(has_down)
        def _():
            for i, (flips, piece) in enumerate(zs):
                act(copy_of(slot(z, *flips), piece, down, send0.at[15 + nz + i]))

    def go(copy):
        copy.start()

    def sent(copy):
        copy.wait_send()

    first_stage(go, first_x, first_y, first_z, 0, 0, 0)
    w_load.start()

    lane = lax.broadcasted_iota(jnp.int32, (1, tiles * LANES), 1) % rows
    span0, span1 = span_ref[2 * me], span_ref[2 * me + 1]
    row_pos = jnp.where(lane < span_len, span0 * span_len + lane, (span1 - 1) * span_len + lane)
    row_pos = row_pos.astype(jnp.float32)
    row_low = jnp.zeros_like(row_pos)
    docs = doc_ref[...]
    for d in range(1, DOCS):
        start = jnp.sum(jnp.where(docs < d, 1.0, 0.0), keepdims=True)
        row_low = jnp.maximum(row_low, jnp.where(start <= row_pos, start, 0.0))
    for c in range(tiles):
        low[c] = row_low[:, c * LANES:(c + 1) * LANES]
        high[c] = row_pos[:, c * LANES:(c + 1) * LANES]
    for g in range(kv_heads):
        heads = [q_ref[:, (g * group + h) * HEAD_WIDTH:(g * group + h + 1) * HEAD_WIDTH] for h in range(group)]
        flipped = jnp.concatenate(heads, axis=0).T
        for c in range(tiles):
            q_t[g, c] = flipped[:, c * LANES:(c + 1) * LANES]

    factor = HEAD_WIDTH ** (-0.5) * math.log2(math.e)

    def attend(src, initial=False):
        s0, s1 = span_ref[2 * src], span_ref[2 * src + 1]
        key = lax.broadcasted_iota(jnp.int32, (rows, LANES), 0)
        key_pos = jnp.where(key < span_len, s0 * span_len, (s1 - 1) * span_len) + key
        key_pos = key_pos.astype(jnp.float32)
        for c in range(tiles):
            visible = (key_pos >= low[c]) & (key_pos <= high[c])
            bias[c] = jnp.where(visible, 0.0, NEG)

        def weigh(g):
            keys = kv[src, 0, :, g * HEAD_WIDTH:(g + 1) * HEAD_WIDTH]
            for c in range(tiles):
                scores = jnp.dot(keys, q_t[g, c], preferred_element_type=jnp.float32)
                scores = scores * factor + bias[c]
                top = jnp.max(scores, axis=0, keepdims=True)
                if not initial:
                    old = best[g, c]
                    top = jnp.maximum(old, top)
                    fade = jnp.exp2(old - top)
                    fades[g, c] = fade
                weights = jnp.exp2(scores - top)
                weight_sum = jnp.sum(weights, axis=0, keepdims=True)
                best[g, c] = top
                total[g, c] = weight_sum if initial else total[g, c] * fade + weight_sum
                held[g, c] = weights.astype(jnp.bfloat16)

        def gather(g):
            values = kv[src, 1, :, g * HEAD_WIDTH:(g + 1) * HEAD_WIDTH].T
            for c in range(tiles):
                part_sum = jnp.dot(values, held[g, c], preferred_element_type=jnp.float32)
                acc[g, c] = part_sum if initial else acc[g, c] * fades[g, c] + part_sum

        for g in range(kv_heads):
            weigh(g)
            if g:
                gather(g - 1)
        gather(kv_heads - 1)

    attend(me, initial=True)

    arrived(slot(z, *xn), "A")
    arrived(slot(z, *yn), "B")
    first_stage(go, [(yn, "B")], [(xn, "A")], later_z, 3, 3, 3)
    arrived(slot(z, *xn), "C")
    arrived(slot(z, *yn), "C")
    first_stage(go, [(yn, "C0")], [(xn, "C1")], [], 4, 4, 0)
    near = jnp.minimum(z, line - 1 - z)

    def plane(j):
        both = jnp.where(j % 2 == 1, z + (j + 1) // 2, z - j // 2)
        rest = jnp.where(z < line - 1 - z, j, line - 1 - j)
        return jnp.where(j <= 2 * near, both, rest)

    def sides(i, fn):
        @pl.when(z - i >= 0)
        def _():
            fn(z - i, 0, has_up, up)

        @pl.when((z + i < line) & (i > 0))
        def _():
            fn(z + i, 1, has_down, down)

    z_pieces = [(own, "C", "xy"), (own, "A", "y"), (own, "B", "x"), (xn, "A", "y"), (yn, "B", "x")]

    def z_step(i, n, act):
        flips, piece, links = z_pieces[n]

        def fn(zz, side, can, target):
            src = slot(zz, *flips)
            if act is go:
                arrived(src, piece)

            @pl.when(can)
            def _():
                act(copy_of(src, piece, target, send_z.at[i - 1, side, n]))

            if "x" in links:
                act(copy_of(src, piece, to_x, send_xy.at[i - 1, side, 0, min(n, 2)
                                                         if n != 4 else 1]))
            if "y" in links:
                act(copy_of(src, piece, to_y, send_xy.at[i - 1, side, 1, min(n, 2)]))

        sides(i, fn)

    def corner_step(i, act):
        def fn(zz, side, can, target):
            src_x, src_y = slot(zz, *xn), slot(zz, *yn)
            if act is go:
                arrived(src_x, "C")
            act(copy_of(src_x, "C1", to_y, send_xy.at[i - 1, side, 1, 3]))
            if act is go:
                arrived(src_y, "C")
            act(copy_of(src_y, "C0", to_x, send_xy.at[i - 1, side, 0, 3]))

        sides(i, fn)

    def wait_step(i, flips, pieces):
        def fn(zz, side, can, target):
            for piece in pieces:
                arrived(slot(zz, *flips), piece)

        sides(i, fn)

    dg_pieces = ("B", "A", "C0", "C1")

    def finish(i):
        here = plane(i)
        for flips, pieces in ((xn, ("B",)), (yn, ("A",)), (dg, dg_pieces)):
            wait_step(i, flips, pieces)
            attend(slot(here, *flips))

    def stage(i, carry, last=False):
        z_step(i, 0, go)
        z_step(i, 1, go)

        @pl.when(i > 1)
        def _():
            corner_step(i - 1, go)

        z_step(i, 2, go)
        if last:
            finish(i - 1)
            attend(slot(plane(i), *own))
        z_step(i, 3, go)
        z_step(i, 4, go)
        if not last:
            attend(slot(plane(i), *own))
            finish(i - 1)
        return carry

    lax.fori_loop(1, line - 1, stage, 0)
    stage(line - 1, 0, last=True)
    corner_step(line - 1, go)
    finish(line - 1)

    for g in range(kv_heads):
        parts = [acc[g, c] / total[g, c] for c in range(tiles)]
        turned = jnp.concatenate(parts, axis=1).T.astype(jnp.bfloat16)
        for h in range(group):
            first = (g * group + h) * HEAD_WIDTH
            attn[:, first:first + HEAD_WIDTH] = turned[h * rows:(h + 1) * rows]

    w_load.wait()
    half = rows // 2
    count, width = outgoing.shape[0], outgoing.shape[2]

    def hand_over(n):
        return pltpu.make_async_remote_copy(
            src_ref=outgoing.at[n], dst_ref=incoming.at[n], send_sem=out_send.at[n],
            recv_sem=out_recv.at[n], device_id={"hd": 1 - hd}, device_id_type=MESH,
        )

    @pl.loop(0, count)
    def _(n):
        columns = pl.ds(pl.multiple_of(n * width, width), width)
        product = jnp.dot(attn[...], w_vmem[:, columns], preferred_element_type=jnp.float32)
        upper, lower = product[:half], product[half:]
        mine = hd == 0
        outgoing[n] = jnp.where(mine, lower, upper).astype(jnp.bfloat16)
        kept[n] = jnp.where(mine, upper, lower)
        hand_over(n).start()

    for n in range(count):
        hand_over(n).wait_recv()
        out_ref[:, n * width:(n + 1) * width] = (kept[n] + incoming[n].astype(jnp.float32)).astype(jnp.bfloat16)

    for n in range(count):
        hand_over(n).wait_send()
    first_stage(sent, first_x, first_y, first_z, 0, 0, 0)
    first_stage(sent, [(yn, "B")], [(xn, "A")], later_z, 3, 3, 3)
    first_stage(sent, [(yn, "C0")], [(xn, "C1")], [], 4, 4, 0)

    def drain(i, carry):
        for n in range(5):
            z_step(i, n, sent)
        corner_step(i, sent)
        return carry

    lax.fori_loop(1, line, drain, 0)


def local(cp, queries, keys, values, span_table, doc_ids, out_weight):
    rows = queries.shape[0]
    kv_heads = keys.shape[1] // HEAD_WIDTH
    group = queries.shape[1] // HEAD_WIDTH // kv_heads
    tiles = group * rows // LANES
    line = cp // 4
    model = out_weight.shape[1]
    count = 8
    width = model // count
    half = rows // 2
    vmem, hbm = pltpu.VMEM, pl.ANY
    spec = lambda space: pl.BlockSpec(memory_space=space)
    dma = pltpu.SemaphoreType.DMA
    f32, bf16 = jnp.float32, jnp.bfloat16
    return pl.pallas_call(
        functools.partial(kernel, line),
        out_shape=jax.ShapeDtypeStruct((half, model), bf16),
        in_specs=[spec(vmem), spec(pltpu.SMEM), spec(vmem), spec(hbm), spec(hbm), spec(hbm)],
        out_specs=spec(vmem),
        scratch_shapes=[
            vmem((cp, 2, rows, keys.shape[1]), bf16),
            vmem(out_weight.shape, bf16),
            vmem((kv_heads, tiles, HEAD_WIDTH, LANES), bf16),
            vmem((kv_heads, tiles, HEAD_WIDTH, LANES), f32),
            vmem((kv_heads, tiles, 1, LANES), f32),
            vmem((kv_heads, tiles, 1, LANES), f32),
            vmem((kv_heads, tiles, 1, LANES), f32),
            vmem((kv_heads, tiles, rows, LANES), bf16),
            vmem((tiles, rows, LANES), f32),
            vmem((tiles, 1, LANES), f32),
            vmem((tiles, 1, LANES), f32),
            vmem((rows, queries.shape[1]), bf16),
            vmem((count, half, width), bf16),
            vmem((count, half, width), bf16),
            vmem((count, half, width), f32),
            dma((2,)), dma, dma((20,)), dma((line, 2, 5)), dma((line, 2, 2, 4)),
            dma((cp, 4)), dma((count,)), dma((count,)),
        ],
        compiler_params=pltpu.CompilerParams(
            collective_id=0, has_side_effects=True, vmem_limit_bytes=60 * 2 ** 20,
        ),
    )(queries, span_table, doc_ids.reshape(-1, 128), keys, values, out_weight)


def solution(mesh):
    return jax.shard_map(
        functools.partial(local, mesh.shape["cp"]),
        mesh=mesh,
        in_specs=(P("cp", "hd"), P("cp", "hd"), P("cp", "hd"), P(), P(), P("hd", None)),
        out_specs=P(("cp", "hd"), None),
        check_vma=False,
    )
```

profile of v0, /device:TPU:0, one launch (start us, length us, event | category | flops | bytes accessed | tf_op | source)
XLA Modules:
  0.0 66.8 jit_solution(5432208706918322097)
XLA Ops:
  0.0 64.7 %shard_map.64 = bf16[96,4096]{1,0:T(8,128)(2,1)} custom-call(bf16[192,2048]{1,0:T(8,128)(2,1)} %q_ref.1, s32[32]{0:T(128)} %span_ref.1, s32[24,128]{1,0:T(8,128)} %bitcast.1, bf16[192,512]{1,0:T(8,128)(2,1)} %k_hbm.1, bf16[192,512]{1,0:T(8,128)(2,1)} %v_hbm.1, bf16[2048,4096]{1,0:T(8,128)(2,1)} %w_hbm.1), custom_call_target="tpu_custom_call" | custom-call | tf_op jit(solution)/shard_map/pallas_call | solution.py:335
  64.7 2.1 %copy.8 = bf16[96,4096]{1,0:T(8,128)(2,1)} copy(bf16[96,4096]{1,0:T(8,128)(2,1)} %shard_map.64) | data formatting | bytes 1572864
where the time goes:
time: 66.9 us; the launch traced here: 66.8 us
  Pallas kernels  64.7 us (97%)
  local copies, waits for them, and re-layouts  2.06 us (3%)
    pallas_call x1, Pallas kernels, local(): pl.pallas_call(functools.partial(kernel, line), out_shape=jax.ShapeDtypeS...  64.7 us
    unnamed x1, local copies, waits for them, and re-layouts  2.06 us

commit v1 on v0

v1 whole, which is shorter than its diff:
```python
import functools
import math

import jax
import jax.numpy as jnp
from jax import lax
from jax.experimental import pallas as pl
from jax.experimental.pallas import tpu as pltpu
from jax.sharding import PartitionSpec as P

HEAD_WIDTH = 128
DOCS = 8
LANES = 256
MATES = 4
NEG = -1e30
MESH = pl.DeviceIdType.MESH
FACTOR = HEAD_WIDTH ** (-0.5) * math.log2(math.e)
f32, bf16 = jnp.float32, jnp.bfloat16


def kernel(
    line, span_ref, doc_ref, q_hbm, k_hbm, v_hbm, w_hbm, out_ref,
    kv, kv_out, q_in, q_out, marks, q_t, acc, best, total, fades, held,
    w_vmem, attn, o_out, outgoing, incoming, kept,
    load_kv, load_q, w_sem, send_kv, send_q, send_o, send_z, recv_kv, recv_q, recv_o, out_send, out_recv,
):
    rows = k_hbm.shape[0]
    span_len = rows // 2
    wide = q_hbm.shape[1] // MATES
    group = wide // HEAD_WIDTH
    tiles = group * rows // LANES
    me = lax.axis_index("cp")
    hd = lax.axis_index("hd")
    z, p = me // MATES, me % MATES
    y, x = p // 2, p % 2
    has_up, has_down = z < line - 1, z > 0
    up, down = me + MATES, me - MATES

    def member(i):
        return (y + (i // 2) * (1 - 2 * y)) * 2 + x + (i % 2) * (1 - 2 * x)

    def mate(i):
        return z * MATES + member(i)

    def columns(i, size):
        return pl.ds(pl.multiple_of(member(i) * size, size), size)

    def kv_load(i, h):
        src = (k_hbm, v_hbm)[h].at[:, columns(i, HEAD_WIDTH)]
        dst = kv.at[me, h] if i == 0 else kv_out.at[i, h]
        return pltpu.make_async_copy(src, dst, load_kv.at[i, h])

    def q_load(i):
        dst = q_in.at[0] if i == 0 else q_out.at[i]
        return pltpu.make_async_copy(q_hbm.at[:, columns(i, wide)], dst, load_q.at[i])

    def w_load(i):
        src = w_hbm.at[pl.ds(pl.multiple_of(member(i) * wide, wide), wide), :]
        return pltpu.make_async_copy(src, w_vmem.at[i * wide:(i + 1) * wide, :], w_sem.at[i])

    def remote(src, dst, send, recv, target):
        return pltpu.make_async_remote_copy(
            src_ref=src, dst_ref=dst, send_sem=send, recv_sem=recv,
            device_id={"cp": target}, device_id_type=MESH,
        )

    def kv_send(i, h):
        return remote(kv_out.at[i, h], kv.at[me, h], send_kv.at[i, h], recv_kv.at[me, h], mate(i))

    def q_send(i):
        return remote(q_out.at[i], q_in.at[i], send_q.at[i], recv_q.at[i], mate(i))

    def o_send(i):
        dst = attn.at[:, pl.ds(pl.multiple_of(i * wide, wide), wide)]
        return remote(o_out.at[i], dst, send_o.at[i], recv_o.at[i], mate(i))

    def z_send(d, side, i, h, src, target):
        block = kv.at[src, h]
        return remote(block, block, send_z.at[d, side, i, h], recv_kv.at[src, h], target)

    def arrived(src):
        for h in range(2):
            remote(kv.at[src, h], kv.at[src, h], send_z.at[0, 0, 0, h], recv_kv.at[src, h], mate(1)).wait_recv()

    for i in range(MATES):
        for h in range(2):
            kv_load(i, h).start()
    for i in range(MATES):
        q_load(i).start()

    barrier = pltpu.get_barrier_semaphore()
    for i in range(1, MATES):
        pl.semaphore_signal(barrier, inc=1, device_id={"cp": mate(i)}, device_id_type=MESH)
    pl.semaphore_signal(barrier, inc=1, device_id={"hd": 1 - hd}, device_id_type=MESH)

    @pl.when(has_up)
    def _():
        pl.semaphore_signal(barrier, inc=1, device_id={"cp": up}, device_id_type=MESH)

    @pl.when(has_down)
    def _():
        pl.semaphore_signal(barrier, inc=1, device_id={"cp": down}, device_id_type=MESH)

    for h in range(2):
        kv_load(0, h).wait()
    pl.semaphore_wait(barrier, MATES + has_up.astype(jnp.int32) + has_down.astype(jnp.int32))

    def own_z(i, h, act):
        @pl.when(has_up)
        def _():
            act(z_send(0, 0, i, h, mate(i), up))

        @pl.when(has_down)
        def _():
            act(z_send(0, 1, i, h, mate(i), down))

    def go(copy):
        copy.start()

    def sent(copy):
        copy.wait_send()

    for h in range(2):
        own_z(0, h, go)
    for i in range(1, MATES):
        for h in range(2):
            kv_load(i, h).wait()
            kv_send(i, h).start()
    for i in range(1, MATES):
        q_load(i).wait()
        q_send(i).start()
    for i in range(MATES):
        w_load(i).start()

    docs = doc_ref[...]
    starts = [jnp.zeros((1, 1), f32)]
    for d in range(1, DOCS):
        starts.append(jnp.sum(jnp.where(docs < d, 1.0, 0.0), keepdims=True))
    starts.append(jnp.full((1, 1), docs.size, f32))
    lane = lax.broadcasted_iota(jnp.int32, (1, HEAD_WIDTH), 1)
    start_row = jnp.full((1, HEAD_WIDTH), 4.0 * docs.size, f32)
    end_row = jnp.full((1, HEAD_WIDTH), 4.0 * docs.size, f32)
    for d in range(DOCS):
        start_row = jnp.where(lane == d, starts[d], start_row)
        end_row = jnp.where(lane == d, starts[d + 1], end_row)
    span_row = jnp.full((1, HEAD_WIDTH), docs.size, jnp.int32)
    for i in range(MATES):
        for s in range(2):
            span_row = jnp.where(lane == DOCS + 2 * i + s, span_ref[2 * mate(i) + s], span_row)

    def mark(src):
        key = lax.broadcasted_iota(jnp.int32, (rows, HEAD_WIDTH), 0)
        first = key < span_len
        span = jnp.where(first, span_ref[2 * src], span_ref[2 * src + 1])
        key_pos = (span * span_len + jnp.where(first, key, key - span_len)).astype(f32)
        of_doc = jnp.where((key_pos >= start_row) & (key_pos < end_row), 1.0, 0.0)
        marks[src] = jnp.where(span > span_row, NEG, of_doc).astype(bf16)

    def q_place(i):
        at = lax.broadcasted_iota(jnp.int32, (1, group * rows), 1) % rows
        s0, s1 = span_ref[2 * mate(i)], span_ref[2 * mate(i) + 1]
        pos = jnp.where(at < span_len, s0 * span_len + at, (s1 - 1) * span_len + at)
        return at, pos.astype(f32)

    def prepare(i):
        heads = [q_in[i, :, h * HEAD_WIDTH:(h + 1) * HEAD_WIDTH] for h in range(group)]
        flipped = jnp.concatenate(heads, axis=0).T
        at, pos = q_place(i)
        row = lax.broadcasted_iota(jnp.int32, (HEAD_WIDTH, group * rows), 0)
        extra = jnp.where(row == DOCS + 2 * i + (at >= span_len).astype(jnp.int32), 1.0, 0.0)
        for d in range(DOCS):
            same = (pos >= starts[d]) & (pos < starts[d + 1])
            extra = jnp.where(row == d, jnp.where(same, 0.0, NEG), extra)
        extra = extra.astype(bf16)
        for c in range(tiles):
            cut = slice(c * LANES, (c + 1) * LANES)
            q_t[i, c, :HEAD_WIDTH] = flipped[:, cut]
            q_t[i, c, HEAD_WIDTH:] = extra[:, cut]
            acc[i, c] = jnp.zeros((HEAD_WIDTH, LANES), f32)
            total[i, c] = jnp.zeros((1, LANES), f32)
            best[i, c] = jnp.full((1, LANES), NEG, f32)

    def attend(i, plane, own=False):
        base = plane * MATES
        if own:
            _, pos = q_place(i)

        def weigh(c):
            parts = []
            for b in range(MATES):
                src = base + b
                keys = jnp.concatenate([kv[src, 0], marks[src]], axis=1)
                scores = jnp.dot(keys, q_t[i, c], preferred_element_type=f32)
                if own:
                    key = lax.broadcasted_iota(jnp.int32, (rows, LANES), 0)
                    key_pos = jnp.where(
                        key < span_len, span_ref[2 * src] * span_len, (span_ref[2 * src + 1] - 1) * span_len
                    ) + key
                    late = key_pos.astype(f32) > pos[:, c * LANES:(c + 1) * LANES]
                    scores = jnp.where(late, NEG, scores)
                parts.append(scores)
            tops = [jnp.max(s, axis=0, keepdims=True) for s in parts]
            old = best[i, c]
            top = functools.reduce(jnp.maximum, tops, old)
            fade = jnp.exp2((old - top) * FACTOR)
            shift = top * FACTOR
            summed = total[i, c] * fade
            for b, scores in enumerate(parts):
                weights = jnp.exp2(scores * FACTOR - shift)
                summed = summed + jnp.sum(weights, axis=0, keepdims=True)
                held[c, b * rows:(b + 1) * rows] = weights.astype(bf16)
            total[i, c] = summed
            best[i, c] = top
            fades[c] = fade

        values = jnp.concatenate([kv[base + b, 1] for b in range(MATES)], axis=0).T

        def gather(c):
            part = jnp.dot(values, held[c], preferred_element_type=f32)
            acc[i, c] = acc[i, c] * fades[c] + part

        for c in range(tiles):
            weigh(c)
            if c:
                gather(c - 1)
        gather(tiles - 1)

    def finalize(i):
        parts = [acc[i, c] / total[i, c] for c in range(tiles)]
        turned = jnp.concatenate(parts, axis=1).T.astype(bf16)
        for h in range(group):
            o_out[i, :, h * HEAD_WIDTH:(h + 1) * HEAD_WIDTH] = turned[h * rows:(h + 1) * rows]

    def forward(d, i):
        for side, plane, more, target in ((0, z - d, has_up, up), (1, z + d, has_down, down)):
            src = plane * MATES + member(i)

            @pl.when((plane >= 0) & (plane < line))
            def _():
                arrived(src)

                @pl.when(more)
                def _():
                    for h in range(2):
                        z_send(d, side, i, h, src, target).start()

    def drained(d, i):
        for side, plane, more, target in ((0, z - d, has_up, up), (1, z + d, has_down, down)):
            src = plane * MATES + member(i)

            @pl.when(jnp.minimum(jnp.minimum(plane, line - 1 - plane), more.astype(jnp.int32) - 1) >= 0)
            def _():
                for h in range(2):
                    z_send(d, side, i, h, src, target).wait_send()

    q_load(0).wait()
    prepare(0)
    for i in range(1, MATES):
        for h in range(2):
            kv_send(i, h).wait_send()
        arrived(mate(i))
        for h in range(2):
            own_z(i, h, go)

    def mark_step(src, carry):
        mark(src)
        return carry

    lax.fori_loop(0, line * MATES, mark_step, 0)
    attend(0, z, own=True)
    for i in range(MATES):
        forward(1, i)

    def own_step(i, carry):
        q_send(i).wait_recv()
        prepare(i)
        attend(i, z, own=True)
        return carry

    lax.fori_loop(1, MATES, own_step, 0)

    furthest = jnp.maximum(z, line - 1 - z)

    def step(n, carry):
        d, k = n // MATES + 1, n % MATES
        i = MATES - 1 - k

        @pl.when(d < line - 1)
        def _():
            forward(d + 1, k)

        def side(s, inner):
            plane = z + d * (2 * s - 1)

            @pl.when((plane >= 0) & (plane < line))
            def _():
                attend(i, plane)

            return inner

        lax.fori_loop(0, 2, side, 0)

        @pl.when(d == furthest)
        def _():
            finalize(i)

            @pl.when(i > 0)
            def _():
                o_send(i).start()

        return carry

    lax.fori_loop(0, (line - 1) * MATES, step, 0)

    attn[:, :wide] = o_out[0]
    for i in range(MATES):
        w_load(i).wait()
    for i in range(1, MATES):
        o_send(i).wait_recv()

    half = rows // 2
    count, width = outgoing.shape[0], outgoing.shape[2]

    def hand_over(n):
        return pltpu.make_async_remote_copy(
            src_ref=outgoing.at[n], dst_ref=incoming.at[n], send_sem=out_send.at[n],
            recv_sem=out_recv.at[n], device_id={"hd": 1 - hd}, device_id_type=MESH,
        )

    @pl.loop(0, count)
    def _(n):
        cols = pl.ds(pl.multiple_of(n * width, width), width)
        product = jnp.dot(attn[...], w_vmem[:, cols], preferred_element_type=f32)
        upper, lower = product[:half], product[half:]
        mine = hd == 0
        outgoing[n] = jnp.where(mine, lower, upper).astype(bf16)
        kept[n] = jnp.where(mine, upper, lower)
        hand_over(n).start()

    for n in range(count):
        hand_over(n).wait_recv()
        out_ref[:, n * width:(n + 1) * width] = (kept[n] + incoming[n].astype(f32)).astype(bf16)

    for n in range(count):
        hand_over(n).wait_send()
    for i in range(1, MATES):
        q_send(i).wait_send()
        o_send(i).wait_send()
    for i in range(MATES):
        for h in range(2):
            own_z(i, h, sent)

    def drain(n, carry):
        drained(n // MATES + 1, n % MATES)
        return carry

    lax.fori_loop(0, (line - 1) * MATES, drain, 0)


def local(cp, queries, keys, values, span_table, doc_ids, out_weight):
    rows = queries.shape[0]
    kv_heads = keys.shape[1] // HEAD_WIDTH
    wide = queries.shape[1] // kv_heads
    tiles = wide // HEAD_WIDTH * rows // LANES
    line = cp // MATES
    model = out_weight.shape[1]
    count = 8
    width = model // count
    half = rows // 2
    vmem, hbm = pltpu.VMEM, pl.ANY
    spec = lambda space: pl.BlockSpec(memory_space=space)
    dma = pltpu.SemaphoreType.DMA
    return pl.pallas_call(
        functools.partial(kernel, line),
        out_shape=jax.ShapeDtypeStruct((half, model), bf16),
        in_specs=[spec(pltpu.SMEM), spec(vmem), spec(hbm), spec(hbm), spec(hbm), spec(hbm)],
        out_specs=spec(vmem),
        scratch_shapes=[
            vmem((cp, 2, rows, HEAD_WIDTH), bf16),
            vmem((MATES, 2, rows, HEAD_WIDTH), bf16),
            vmem((MATES, rows, wide), bf16),
            vmem((MATES, rows, wide), bf16),
            vmem((cp, rows, HEAD_WIDTH), bf16),
            vmem((MATES, tiles, 2 * HEAD_WIDTH, LANES), bf16),
            vmem((MATES, tiles, HEAD_WIDTH, LANES), f32),
            vmem((MATES, tiles, 1, LANES), f32),
            vmem((MATES, tiles, 1, LANES), f32),
            vmem((tiles, 1, LANES), f32),
            vmem((tiles, MATES * rows, LANES), bf16),
            vmem(out_weight.shape, bf16),
            vmem((rows, MATES * wide), bf16),
            vmem((MATES, rows, wide), bf16),
            vmem((count, half, width), bf16),
            vmem((count, half, width), bf16),
            vmem((count, half, width), f32),
            dma((MATES, 2)), dma((MATES,)), dma((MATES,)), dma((MATES, 2)), dma((MATES,)), dma((MATES,)),
            dma((line, 2, MATES, 2)), dma((cp, 2)), dma((MATES,)), dma((MATES,)), dma((count,)), dma((count,)),
        ],
        compiler_params=pltpu.CompilerParams(
            collective_id=0, has_side_effects=True, vmem_limit_bytes=62 * 2 ** 20,
        ),
    )(span_table, doc_ids.reshape(-1, 128), queries, keys, values, out_weight)


def solution(mesh):
    return jax.shard_map(
        functools.partial(local, mesh.shape["cp"]),
        mesh=mesh,
        in_specs=(P("cp", "hd"), P("cp", "hd"), P("cp", "hd"), P(), P(), P("hd", None)),
        out_specs=P(("cp", "hd"), None),
        check_vma=False,
    )
```

time: 66.9 us -> 55.2 us (0.83)
  Pallas kernels: 64.7 us -> 52.9 us
    pallas_call x1, Pallas kernels: 64.7 us -> 52.9 us  [local(): pl.pallas_call(functools.partial(kernel, line), out_shape=jax.ShapeDtypeS...]
where the time goes in v1:
time: 55.2 us; the launch traced here: 55 us
  Pallas kernels  52.9 us (96%)
  local copies, waits for them, and re-layouts  2.06 us (4%)
    pallas_call x1, Pallas kernels, local(): pl.pallas_call(functools.partial(kernel, line), out_shape=jax.ShapeDtypeS...  52.9 us
    unnamed x1, local copies, waits for them, and re-layouts  2.06 us

profile of v1, /device:TPU:0, one launch (start us, length us, event | category | flops | bytes accessed | tf_op | source)
XLA Modules:
  0.0 55.0 jit_solution(4809868045648088462)
XLA Ops:
  0.0 52.9 %shard_map.64 = bf16[96,4096]{1,0:T(8,128)(2,1)} custom-call(s32[32]{0:T(128)} %span_ref.1, s32[24,128]{1,0:T(8,128)} %bitcast.1, bf16[192,2048]{1,0:T(8,128)(2,1)} %q_hbm.1, bf16[192,512]{1,0:T(8,128)(2,1)} %k_hbm.1, bf16[192,512]{1,0:T(8,128)(2,1)} %v_hbm.1, bf16[2048,4096]{1,0:T(8,128)(2,1)} %w_hbm.1), custom_call_target="tpu_custom_call" | custom-call | tf_op jit(solution)/shard_map/pallas_call | solution.py:373
  52.9 2.1 %copy.8 = bf16[96,4096]{1,0:T(8,128)(2,1)} copy(bf16[96,4096]{1,0:T(8,128)(2,1)} %shard_map.64) | data formatting | bytes 1572864

commit v2 on v1

v2 whole, which is shorter than its diff:
```python
import functools
import math

import jax
import jax.numpy as jnp
from jax import lax
from jax.experimental import pallas as pl
from jax.experimental.pallas import tpu as pltpu
from jax.sharding import PartitionSpec as P

HEAD_WIDTH = 128
DOCS = 8
MATES = 4
DOCUMENT_SHARE = 4
NEG = -1e30
MESH = pl.DeviceIdType.MESH
FACTOR = HEAD_WIDTH ** (-0.5) * math.log2(math.e)
f32, bf16 = jnp.float32, jnp.bfloat16


def kernel(
    line, span_ref, doc_ref, q_hbm, k_hbm, v_hbm, w_hbm, out_ref,
    kv, kv_out, q_in, q_out, marks, q_t, slot_of, k_near, v_near, raw, held,
    w_vmem, attn, o_out, partial, outgoing, incoming, kept,
    load_kv, load_q, w_sem, send_kv, send_q, send_o, send_z, recv_kv, recv_q, recv_o, out_send, out_recv, turn,
):
    rows = k_hbm.shape[0]
    span_len = rows // 2
    wide = q_hbm.shape[1] // MATES
    group = wide // HEAD_WIDTH
    slots = span_ref.shape[0]
    reach = k_near.shape[1] // span_len
    me = lax.axis_index("cp")
    hd = lax.axis_index("hd")
    z, p = me // MATES, me % MATES
    y, x = p // 2, p % 2
    has_up, has_down = z < line - 1, z > 0
    up, down = me + MATES, me - MATES

    def member(i):
        return (y + (i // 2) * (1 - 2 * y)) * 2 + x + (i % 2) * (1 - 2 * x)

    def mate(i):
        return z * MATES + member(i)

    def columns(i, size):
        return pl.ds(pl.multiple_of(member(i) * size, size), size)

    class kv_load:
        def __init__(self, i, h):
            spot = kv.at[me, h] if i == 0 else kv_out.at[i, h]
            self.copies = [
                pltpu.make_async_copy(
                    (k_hbm, v_hbm)[h].at[s * span_len:(s + 1) * span_len, columns(i, HEAD_WIDTH)],
                    spot.at[s], load_kv.at[i, h, s],
                )
                for s in range(2)
            ]

        def start(self):
            for copy in self.copies:
                copy.start()

        def wait(self):
            for copy in self.copies:
                copy.wait()

    def q_load(i):
        dst = q_in.at[0] if i == 0 else q_out.at[i]
        return pltpu.make_async_copy(q_hbm.at[:, columns(i, wide)], dst, load_q.at[i])

    def w_load(i):
        src = w_hbm.at[pl.ds(pl.multiple_of(member(i) * wide, wide), wide), :]
        return pltpu.make_async_copy(src, w_vmem.at[i * wide:(i + 1) * wide, :], w_sem.at[i])

    def remote(src, dst, send, recv, target):
        return pltpu.make_async_remote_copy(
            src_ref=src, dst_ref=dst, send_sem=send, recv_sem=recv,
            device_id={"cp": target}, device_id_type=MESH,
        )

    def kv_send(i, h):
        return remote(kv_out.at[i, h], kv.at[me, h], send_kv.at[i, h], recv_kv.at[me, h], mate(i))

    def q_send(i):
        return remote(q_out.at[i], q_in.at[i], send_q.at[i], recv_q.at[i], mate(i))

    def o_send(i):
        dst = attn.at[:, pl.ds(pl.multiple_of(i * wide, wide), wide)]
        return remote(o_out.at[i], dst, send_o.at[i], recv_o.at[i], mate(i))

    def z_send(d, side, i, h, src, target):
        block = kv.at[src, h]
        return remote(block, block, send_z.at[d, side, i, h], recv_kv.at[src, h], target)

    def z_block(d, side, i, src, target):
        return remote(kv.at[src], kv.at[src], send_z.at[d, side, i, 0], recv_kv.at[src, 0], target)

    def arrived(d, src):
        @pl.when(d == 1)
        def _():
            for h in range(2):
                remote(kv.at[src, h], kv.at[src, h], send_z.at[0, 0, 0, h], recv_kv.at[src, h], mate(1)).wait_recv()

        @pl.when(d > 1)
        def _():
            z_block(0, 0, 0, src, mate(1)).wait_recv()

    for i in range(MATES):
        for h in range(2):
            kv_load(i, h).start()
    for i in range(MATES):
        q_load(i).start()

    barrier = pltpu.get_barrier_semaphore()
    for i in range(1, MATES):
        pl.semaphore_signal(barrier, inc=1, device_id={"cp": mate(i)}, device_id_type=MESH)
    pl.semaphore_signal(barrier, inc=1, device_id={"hd": 1 - hd}, device_id_type=MESH)

    @pl.when(has_up)
    def _():
        pl.semaphore_signal(barrier, inc=1, device_id={"cp": up}, device_id_type=MESH)

    @pl.when(has_down)
    def _():
        pl.semaphore_signal(barrier, inc=1, device_id={"cp": down}, device_id_type=MESH)

    for h in range(2):
        kv_load(0, h).wait()
    pl.semaphore_wait(barrier, MATES + has_up.astype(jnp.int32) + has_down.astype(jnp.int32))

    def own_z(i, h, act):
        @pl.when(has_up)
        def _():
            act(z_send(0, 0, i, h, mate(i), up))

        @pl.when(has_down)
        def _():
            act(z_send(0, 1, i, h, mate(i), down))

    def go(copy):
        copy.start()

    def sent(copy):
        copy.wait_send()

    for h in range(2):
        own_z(0, h, go)
    for i in range(1, MATES):
        for h in range(2):
            kv_load(i, h).wait()
            kv_send(i, h).start()

    def send_queries():
        for i in range(1, MATES):
            q_load(i).wait()
            q_send(i).start()

    @pl.when(hd == 0)
    def _():
        send_queries()


    docs = doc_ref[...]
    starts = [jnp.zeros((1, 1), f32)]
    for d in range(1, DOCS):
        starts.append(jnp.sum(jnp.where(docs < d, 1.0, 0.0), keepdims=True))
    starts.append(jnp.full((1, 1), docs.size, f32))
    lane = lax.broadcasted_iota(jnp.int32, (1, HEAD_WIDTH), 1)
    start_row = jnp.full((1, HEAD_WIDTH), 4.0 * docs.size, f32)
    end_row = jnp.full((1, HEAD_WIDTH), 4.0 * docs.size, f32)
    for d in range(DOCS):
        start_row = jnp.where(lane == d, starts[d], start_row)
        end_row = jnp.where(lane == d, starts[d + 1], end_row)
    void = jnp.where(lane == DOCS, NEG, 0.0)
    marks[slots] = jnp.broadcast_to(void, (span_len, HEAD_WIDTH)).astype(bf16)

    def mark(slot, carry):
        key = lax.broadcasted_iota(jnp.int32, (span_len, HEAD_WIDTH), 0)
        key_pos = (span_ref[slot] * span_len + key).astype(f32)
        of_doc = jnp.where((key_pos >= start_row) & (key_pos < end_row), 1.0, 0.0)
        marks[slot] = of_doc.astype(bf16)
        found = 0
        for other in range(slots):
            found = jnp.maximum(found, jnp.where(span_ref[other] == slot, other, 0))
        slot_of[slot] = found
        return carry

    lanes = group * span_len

    def prepare(i):
        at = lax.broadcasted_iota(jnp.int32, (1, lanes), 1) % span_len
        row = lax.broadcasted_iota(jnp.int32, (HEAD_WIDTH, lanes), 0)
        for s in range(2):
            heads = [
                q_in[i, s * span_len:(s + 1) * span_len, h * HEAD_WIDTH:(h + 1) * HEAD_WIDTH]
                for h in range(group)
            ]
            pos = (span_ref[2 * mate(i) + s] * span_len + at).astype(f32)
            extra = jnp.where(row == DOCS, 1.0, 0.0)
            for d in range(DOCS):
                same = (pos >= starts[d]) & (pos < starts[d + 1])
                extra = jnp.where(row == d, jnp.where(same, 0.0, NEG), extra)
            q_t[2 * i + s, :HEAD_WIDTH] = jnp.concatenate(heads, axis=0).T
            q_t[2 * i + s, HEAD_WIDTH:] = extra.astype(bf16)

    turns = [(i, s) for i in (3, 1, 2, 0) for s in range(2)]
    tops = {}

    def collect(j):
        i, s = turns[j]
        last = span_ref[2 * mate(i) + s]
        for k in range(reach):
            span = last - (reach - 1) + k
            slot = slot_of[jnp.maximum(span, 0)]
            cut = slice(k * span_len, (k + 1) * span_len)
            k_near[j % 2, cut, :HEAD_WIDTH] = kv[slot // 2, 0, slot % 2]
            k_near[j % 2, cut, HEAD_WIDTH:] = marks[jnp.where(span >= 0, slot, slots)]
            v_near[j % 2, cut] = kv[slot // 2, 1, slot % 2]

    def score(j):
        i, s = turns[j]
        scores = jnp.dot(k_near[j % 2], q_t[2 * i + s], preferred_element_type=f32)
        edge = (reach - 1) * span_len
        key = lax.broadcasted_iota(jnp.int32, (span_len, lanes), 0)
        at = lax.broadcasted_iota(jnp.int32, (span_len, lanes), 1) % span_len
        corner = jnp.where(key > at, NEG, scores[edge:])
        raw[j % 2, :edge] = scores[:edge]
        raw[j % 2, edge:] = corner
        top = jnp.max(corner, axis=0, keepdims=True)
        tops[j] = jnp.maximum(top, jnp.max(scores[:edge], axis=0, keepdims=True))

    def weigh(j):
        weights = jnp.exp2(raw[j % 2] * FACTOR - tops[j] * FACTOR)
        tops[j] = 1.0 / jnp.sum(weights, axis=0, keepdims=True)
        held[j % 2] = weights.astype(bf16)

    def blend(j):
        i, s = turns[j]
        mixed = jnp.dot(v_near[j % 2].T, held[j % 2], preferred_element_type=f32)
        turned = (mixed * tops[j]).astype(bf16).T
        for h in range(group):
            o_out[i, s * span_len:(s + 1) * span_len, h * HEAD_WIDTH:(h + 1) * HEAD_WIDTH] = (
                turned[h * span_len:(h + 1) * span_len]
            )
        if s and i:
            o_send(i).start()

    ways = ((0, -1, z, has_up, up), (1, 1, line - 1 - z, has_down, down))

    def forward(d, i):
        for side, sign, last, more, target in ways:
            src = (z + sign * d) * MATES + member(i)

            @pl.when(d <= last)
            def _():
                arrived(d, src)

                @pl.when(more)
                def _():
                    z_block(d, side, i, src, target).start()

    def await_turn():
        for side, sign, last, more, target in ways:

            @pl.when(jnp.minimum(last, more.astype(jnp.int32)) > 0)
            def _():
                pl.semaphore_wait(turn.at[side], 1)

    def give_turn(d):
        for side, sign, last, more, target in ways:
            src = (z + sign * d) * MATES + member(MATES - 1)

            @pl.when((last == d) & more)
            def _():
                z_block(d, side, MATES - 1, src, target).wait_send()
                pl.semaphore_signal(turn.at[side], inc=1, device_id={"hd": 1 - hd}, device_id_type=MESH)

    def drained(d, i):
        for side, sign, last, more, target in ways:
            src = (z + sign * d) * MATES + member(i)
            waited = jnp.maximum(jnp.maximum(hd, MATES - 1 - i), last - d) == 0

            @pl.when((d <= last) & more & jnp.logical_not(waited))
            def _():
                z_block(d, side, i, src, target).wait_send()

    def pass_on(i, h):
        src = mate(i)
        remote(kv.at[src, h], kv.at[src, h], send_z.at[0, 0, 0, h], recv_kv.at[src, h], src).wait_recv()
        own_z(i, h, go)

    def relay(n, carry):
        forward(n // MATES + 1, n % MATES)
        return carry

    for h in range(2):
        pass_on(1, h)
        pass_on(2, h)
    for i in range(MATES):
        w_load(i).start()
    for h in range(2):
        pass_on(3, h)

    @pl.when(hd == 0)
    def _():
        lax.fori_loop(0, (line - 1) * MATES, relay, 0)
        for d in range(1, line):
            give_turn(d)

    @pl.when(hd == 1)
    def _():
        send_queries()

    lax.fori_loop(0, slots, mark, 0)
    q_load(0).wait()
    prepare(0)
    for i in range(1, MATES):
        q_send(i).wait_recv()
        prepare(i)

    @pl.when(hd == 1)
    def _():
        await_turn()
        lax.fori_loop(0, (line - 1) * MATES, relay, 0)

    collect(0)
    score(0)
    for j in range(len(turns)):
        if j + 1 < len(turns):
            collect(j + 1)
            score(j + 1)
        weigh(j)
        blend(j)

    attn[:, :wide] = o_out[0]
    for i in range(MATES):
        w_load(i).wait()

    half = rows // 2
    count, width = outgoing.shape[0], outgoing.shape[2]

    def hand_over(n):
        return pltpu.make_async_remote_copy(
            src_ref=outgoing.at[n], dst_ref=incoming.at[n], send_sem=out_send.at[n],
            recv_sem=out_recv.at[n], device_id={"hd": 1 - hd}, device_id_type=MESH,
        )

    def project(n, i):
        cut = slice(i * wide, (i + 1) * wide)
        return jnp.dot(attn[:, cut], w_vmem[cut, n * width:(n + 1) * width], preferred_element_type=f32)

    for n in range(count):
        partial[n] = project(n, 0)
    for i in (3, 1):
        o_send(i).wait_recv()
        for n in range(count):
            partial[n] += project(n, i)
    o_send(2).wait_recv()
    mine = hd == 0
    for n in range(count):
        product = partial[n] + project(n, 2)
        upper, lower = product[:half], product[half:]
        outgoing[n] = jnp.where(mine, lower, upper).astype(bf16)
        kept[n] = jnp.where(mine, upper, lower)
        hand_over(n).start()

    for n in range(count):
        hand_over(n).wait_recv()
        out_ref[:, n * width:(n + 1) * width] = (kept[n] + incoming[n].astype(f32)).astype(bf16)

    for n in range(count):
        hand_over(n).wait_send()
    for i in range(1, MATES):
        for h in range(2):
            kv_send(i, h).wait_send()
        q_send(i).wait_send()
        o_send(i).wait_send()
    for i in range(MATES):
        for h in range(2):
            own_z(i, h, sent)

    def drain(n, carry):
        drained(n // MATES + 1, n % MATES)
        return carry

    lax.fori_loop(0, (line - 1) * MATES, drain, 0)


def local(cp, queries, keys, values, span_table, doc_ids, out_weight):
    rows = queries.shape[0]
    kv_heads = keys.shape[1] // HEAD_WIDTH
    wide = queries.shape[1] // kv_heads
    slots = span_table.shape[0]
    span_len = rows // 2
    lanes = wide // HEAD_WIDTH * span_len
    near = (slots // DOCUMENT_SHARE + 1) * span_len
    line = cp // MATES
    model = out_weight.shape[1]
    count = 8
    width = model // count
    half = rows // 2
    vmem, hbm = pltpu.VMEM, pl.ANY
    spec = lambda space: pl.BlockSpec(memory_space=space)
    dma = pltpu.SemaphoreType.DMA
    return pl.pallas_call(
        functools.partial(kernel, line),
        out_shape=jax.ShapeDtypeStruct((half, model), bf16),
        in_specs=[spec(pltpu.SMEM), spec(vmem), spec(hbm), spec(hbm), spec(hbm), spec(hbm)],
        out_specs=spec(vmem),
        scratch_shapes=[
            vmem((cp, 2, 2, span_len, HEAD_WIDTH), bf16),
            vmem((MATES, 2, 2, span_len, HEAD_WIDTH), bf16),
            vmem((MATES, rows, wide), bf16),
            vmem((MATES, rows, wide), bf16),
            vmem((slots + 1, span_len, HEAD_WIDTH), bf16),
            vmem((2 * MATES, 2 * HEAD_WIDTH, lanes), bf16),
            pltpu.SMEM((slots,), jnp.int32),
            vmem((2, near, 2 * HEAD_WIDTH), bf16),
            vmem((2, near, HEAD_WIDTH), bf16),
            vmem((2, near, lanes), f32),
            vmem((2, near, lanes), bf16),
            vmem(out_weight.shape, bf16),
            vmem((rows, MATES * wide), bf16),
            vmem((MATES, rows, wide), bf16),
            vmem((count, rows, width), f32),
            vmem((count, half, width), bf16),
            vmem((count, half, width), bf16),
            vmem((count, half, width), f32),
            dma((MATES, 2, 2)), dma((MATES,)), dma((MATES,)), dma((MATES, 2)), dma((MATES,)), dma((MATES,)),
            dma((line, 2, MATES, 2)), dma((cp, 2)), dma((MATES,)), dma((MATES,)), dma((count,)), dma((count,)),
            pltpu.SemaphoreType.REGULAR((2,)),
        ],
        compiler_params=pltpu.CompilerParams(
            collective_id=0, has_side_effects=True, vmem_limit_bytes=62 * 2 ** 20,
        ),
    )(span_table, doc_ids.reshape(-1, 128), queries, keys, values, out_weight)


def solution(mesh):
    return jax.shard_map(
        functools.partial(local, mesh.shape["cp"]),
        mesh=mesh,
        in_specs=(P("cp", "hd"), P("cp", "hd"), P("cp", "hd"), P(), P(), P("hd", None)),
        out_specs=P(("cp", "hd"), None),
        check_vma=False,
    )
```

time: 55.2 us -> 51.3 us (0.929)
  Pallas kernels: 52.9 us -> 49 us
    pallas_call x1, Pallas kernels: 52.9 us -> 49 us  [local(): pl.pallas_call(functools.partial(kernel, line), out_shape=jax.ShapeDtypeS...]
where the time goes in v2:
time: 51.3 us; the launch traced here: 51 us
  Pallas kernels  49 us (96%)
  local copies, waits for them, and re-layouts  2.06 us (4%)
    pallas_call x1, Pallas kernels, local(): pl.pallas_call(functools.partial(kernel, line), out_shape=jax.ShapeDtypeS...  49 us
    unnamed x1, local copies, waits for them, and re-layouts  2.06 us

profile of v2, /device:TPU:0, one launch (start us, length us, event | category | flops | bytes accessed | tf_op | source)
XLA Modules:
  0.0 51.0 jit_solution(1019931224910443270)
XLA Ops:
  0.0 49.0 %shard_map.64 = bf16[96,4096]{1,0:T(8,128)(2,1)} custom-call(s32[32]{0:T(128)} %span_ref.1, s32[24,128]{1,0:T(8,128)} %bitcast.1, bf16[192,2048]{1,0:T(8,128)(2,1)} %q_hbm.1, bf16[192,512]{1,0:T(8,128)(2,1)} %k_hbm.1, bf16[192,512]{1,0:T(8,128)(2,1)} %v_hbm.1, bf16[2048,4096]{1,0:T(8,128)(2,1)} %w_hbm.1), custom_call_target="tpu_custom_call" | custom-call | tf_op jit(solution)/shard_map/pallas_call | solution.py:406
  49.0 2.1 %copy.8 = bf16[96,4096]{1,0:T(8,128)(2,1)} copy(bf16[96,4096]{1,0:T(8,128)(2,1)} %shard_map.64) | data formatting | bytes 1572864

commit v3 on v2

--- a/solution.py
+++ b/solution.py
@@ -19,10 +19,10 @@
 
 
 def kernel(
-    line, span_ref, doc_ref, q_hbm, k_hbm, v_hbm, w_hbm, out_ref,
+    line, span_ref, doc_ref, q_hbm, k_hbm, v_hbm, w_hbm, out_hbm,
     kv, kv_out, q_in, q_out, marks, q_t, slot_of, k_near, v_near, raw, held,
-    w_vmem, attn, o_out, partial, outgoing, incoming, kept,
-    load_kv, load_q, w_sem, send_kv, send_q, send_o, send_z, recv_kv, recv_q, recv_o, out_send, out_recv, turn,
+    w_vmem, attn, o_out, partial, outgoing, incoming, kept, ready,
+    load_kv, load_q, w_sem, send_kv, send_q, send_o, send_z, recv_kv, recv_q, recv_o, out_send, out_recv, out_sem, turn,
 ):
     rows = k_hbm.shape[0]
     span_len = rows // 2
@@ -71,7 +71,7 @@
 
     def w_load(i):
         src = w_hbm.at[pl.ds(pl.multiple_of(member(i) * wide, wide), wide), :]
-        return pltpu.make_async_copy(src, w_vmem.at[i * wide:(i + 1) * wide, :], w_sem.at[i])
+        return pltpu.make_async_copy(src, w_vmem.at[place[i] * wide:(place[i] + 1) * wide, :], w_sem.at[i])
 
     def remote(src, dst, send, recv, target):
         return pltpu.make_async_remote_copy(
@@ -85,9 +85,12 @@
     def q_send(i):
         return remote(q_out.at[i], q_in.at[i], send_q.at[i], recv_q.at[i], mate(i))
 
-    def o_send(i):
-        dst = attn.at[:, pl.ds(pl.multiple_of(i * wide, wide), wide)]
-        return remote(o_out.at[i], dst, send_o.at[i], recv_o.at[i], mate(i))
+    place = (0, 2, 3, 1)
+
+    def o_send(i, s):
+        start = s * span_len if isinstance(s, int) else pl.multiple_of(s * span_len, span_len)
+        dst = attn.at[pl.ds(start, span_len), place[i] * wide:(place[i] + 1) * wide]
+        return remote(o_out.at[i, s], dst, send_o.at[i, s], recv_o.at[i, s], mate(i))
 
     def z_send(d, side, i, h, src, target):
         block = kv.at[src, h]
@@ -216,7 +219,7 @@
             cut = slice(k * span_len, (k + 1) * span_len)
             k_near[j % 2, cut, :HEAD_WIDTH] = kv[slot // 2, 0, slot % 2]
             k_near[j % 2, cut, HEAD_WIDTH:] = marks[jnp.where(span >= 0, slot, slots)]
-            v_near[j % 2, cut] = kv[slot // 2, 1, slot % 2]
+            v_near[j % 3, cut] = kv[slot // 2, 1, slot % 2]
 
     def score(j):
         i, s = turns[j]
@@ -237,14 +240,16 @@
 
     def blend(j):
         i, s = turns[j]
-        mixed = jnp.dot(v_near[j % 2].T, held[j % 2], preferred_element_type=f32)
+        mixed = jnp.dot(v_near[j % 3].T, held[j % 2], preferred_element_type=f32)
         turned = (mixed * tops[j]).astype(bf16).T
         for h in range(group):
-            o_out[i, s * span_len:(s + 1) * span_len, h * HEAD_WIDTH:(h + 1) * HEAD_WIDTH] = (
-                turned[h * span_len:(h + 1) * span_len]
-            )
-        if s and i:
-            o_send(i).start()
+            cut = slice(h * HEAD_WIDTH, (h + 1) * HEAD_WIDTH)
+            if i:
+                o_out[i, s, :, cut] = turned[h * span_len:(h + 1) * span_len]
+            else:
+                attn[s * span_len:(s + 1) * span_len, cut] = turned[h * span_len:(h + 1) * span_len]
+        if i:
+            o_send(i, s).start()
 
     ways = ((0, -1, z, has_up, up), (1, 1, line - 1 - z, has_down, down))
 
@@ -269,19 +274,16 @@
 
     def give_turn(d):
         for side, sign, last, more, target in ways:
-            src = (z + sign * d) * MATES + member(MATES - 1)
 
             @pl.when((last == d) & more)
             def _():
-                z_block(d, side, MATES - 1, src, target).wait_send()
                 pl.semaphore_signal(turn.at[side], inc=1, device_id={"hd": 1 - hd}, device_id_type=MESH)
 
     def drained(d, i):
         for side, sign, last, more, target in ways:
             src = (z + sign * d) * MATES + member(i)
-            waited = jnp.maximum(jnp.maximum(hd, MATES - 1 - i), last - d) == 0
-
-            @pl.when((d <= last) & more & jnp.logical_not(waited))
+
+            @pl.when((d <= last) & more)
             def _():
                 z_block(d, side, i, src, target).wait_send()
 
@@ -304,9 +306,16 @@
 
     @pl.when(hd == 0)
     def _():
-        lax.fori_loop(0, (line - 1) * MATES, relay, 0)
-        for d in range(1, line):
-            give_turn(d)
+        def lead(n, carry):
+            relay(n, carry)
+
+            @pl.when(n % MATES == MATES - 1)
+            def _():
+                give_turn(n // MATES + 1)
+
+            return carry
+
+        lax.fori_loop(0, (line - 1) * MATES, lead, 0)
 
     @pl.when(hd == 1)
     def _():
@@ -324,16 +333,15 @@
         await_turn()
         lax.fori_loop(0, (line - 1) * MATES, relay, 0)
 
-    collect(0)
-    score(0)
-    for j in range(len(turns)):
-        if j + 1 < len(turns):
-            collect(j + 1)
-            score(j + 1)
-        weigh(j)
-        blend(j)
-
-    attn[:, :wide] = o_out[0]
+    for t in range(len(turns) + 2):
+        if t < len(turns):
+            collect(t)
+            score(t)
+        if 1 <= t <= len(turns):
+            weigh(t - 1)
+        if t >= 2:
+            blend(t - 2)
+
     for i in range(MATES):
         w_load(i).wait()
 
@@ -346,28 +354,35 @@
             recv_sem=out_recv.at[n], device_id={"hd": 1 - hd}, device_id_type=MESH,
         )
 
-    def project(n, i):
-        cut = slice(i * wide, (i + 1) * wide)
-        return jnp.dot(attn[:, cut], w_vmem[cut, n * width:(n + 1) * width], preferred_element_type=f32)
-
-    for n in range(count):
-        partial[n] = project(n, 0)
-    for i in (3, 1):
-        o_send(i).wait_recv()
-        for n in range(count):
-            partial[n] += project(n, i)
-    o_send(2).wait_recv()
-    mine = hd == 0
-    for n in range(count):
-        product = partial[n] + project(n, 2)
-        upper, lower = product[:half], product[half:]
-        outgoing[n] = jnp.where(mine, lower, upper).astype(bf16)
-        kept[n] = jnp.where(mine, upper, lower)
+    def store(n):
+        return pltpu.make_async_copy(
+            ready.at[n], out_hbm.at[:, n * width:(n + 1) * width], out_sem.at[n]
+        )
+
+    def project(n, rest, lines):
+        cut = slice(2 * wide, 4 * wide) if rest else slice(0, 2 * wide)
+        return jnp.dot(attn[lines, cut], w_vmem[cut, n * width:(n + 1) * width], preferred_element_type=f32)
+
+    for s in range(2):
+        o_send(3, s).wait_recv()
+    for n in range(count):
+        partial[n] = project(n, False, slice(None))
+    theirs, ours = [pl.ds(pl.multiple_of(s * half, half), half) for s in (1 - hd, hd)]
+    for i in (1, 2):
+        o_send(i, 1 - hd).wait_recv()
+    for n in range(count):
+        outgoing[n] = (partial[n, theirs] + project(n, True, theirs)).astype(bf16)
         hand_over(n).start()
-
+    for i in (1, 2):
+        o_send(i, hd).wait_recv()
+    for n in range(count):
+        kept[n] = partial[n, ours] + project(n, True, ours)
     for n in range(count):
         hand_over(n).wait_recv()
-        out_ref[:, n * width:(n + 1) * width] = (kept[n] + incoming[n].astype(f32)).astype(bf16)
+        ready[n] = (kept[n] + incoming[n].astype(f32)).astype(bf16)
+        store(n).start()
+    for n in range(count):
+        store(n).wait()
 
     for n in range(count):
         hand_over(n).wait_send()
@@ -375,7 +390,8 @@
         for h in range(2):
             kv_send(i, h).wait_send()
         q_send(i).wait_send()
-        o_send(i).wait_send()
+        for s in range(2):
+            o_send(i, s).wait_send()
     for i in range(MATES):
         for h in range(2):
             own_z(i, h, sent)
@@ -407,7 +423,7 @@
         functools.partial(kernel, line),
         out_shape=jax.ShapeDtypeStruct((half, model), bf16),
         in_specs=[spec(pltpu.SMEM), spec(vmem), spec(hbm), spec(hbm), spec(hbm), spec(hbm)],
-        out_specs=spec(vmem),
+        out_specs=spec(hbm),
         scratch_shapes=[
             vmem((cp, 2, 2, span_len, HEAD_WIDTH), bf16),
             vmem((MATES, 2, 2, span_len, HEAD_WIDTH), bf16),
@@ -417,18 +433,19 @@
             vmem((2 * MATES, 2 * HEAD_WIDTH, lanes), bf16),
             pltpu.SMEM((slots,), jnp.int32),
             vmem((2, near, 2 * HEAD_WIDTH), bf16),
-            vmem((2, near, HEAD_WIDTH), bf16),
+            vmem((3, near, HEAD_WIDTH), bf16),
             vmem((2, near, lanes), f32),
             vmem((2, near, lanes), bf16),
             vmem(out_weight.shape, bf16),
             vmem((rows, MATES * wide), bf16),
-            vmem((MATES, rows, wide), bf16),
+            vmem((MATES, 2, span_len, wide), bf16),
             vmem((count, rows, width), f32),
             vmem((count, half, width), bf16),
             vmem((count, half, width), bf16),
             vmem((count, half, width), f32),
-            dma((MATES, 2, 2)), dma((MATES,)), dma((MATES,)), dma((MATES, 2)), dma((MATES,)), dma((MATES,)),
-            dma((line, 2, MATES, 2)), dma((cp, 2)), dma((MATES,)), dma((MATES,)), dma((count,)), dma((count,)),
+            vmem((count, half, width), bf16),
+            dma((MATES, 2, 2)), dma((MATES,)), dma((MATES,)), dma((MATES, 2)), dma((MATES,)), dma((MATES, 2)),
+            dma((line, 2, MATES, 2)), dma((cp, 2)), dma((MATES,)), dma((MATES, 2)), dma((count,)), dma((count,)), dma((count,)),
             pltpu.SemaphoreType.REGULAR((2,)),
         ],
         compiler_params=pltpu.CompilerParams(

time: 51.3 us -> 50 us (0.975)
  Pallas kernels: 49 us -> 47.6 us
    pallas_call x1, Pallas kernels: 49 us -> 47.6 us  [local(): pl.pallas_call(functools.partial(kernel, line), out_shape=jax.ShapeDtypeS...]
where the time goes in v3:
time: 50 us; the launch traced here: 49.7 us
  Pallas kernels  47.6 us (95%)
  local copies, waits for them, and re-layouts  2.06 us (4%)
    pallas_call x1, Pallas kernels, local(): pl.pallas_call(functools.partial(kernel, line), out_shape=jax.ShapeDtypeS...  47.6 us
    unnamed x1, local copies, waits for them, and re-layouts  2.06 us

profile of v3, /device:TPU:0, one launch (start us, length us, event | category | flops | bytes accessed | tf_op | source)
XLA Modules:
  0.0 49.7 jit_solution(12320325477245773621)
XLA Ops:
  0.0 47.6 %shard_map.64 = bf16[96,4096]{1,0:T(8,128)(2,1)} custom-call(s32[32]{0:T(128)} %span_ref.1, s32[24,128]{1,0:T(8,128)} %bitcast.1, bf16[192,2048]{1,0:T(8,128)(2,1)} %q_hbm.1, bf16[192,512]{1,0:T(8,128)(2,1)} %k_hbm.1, bf16[192,512]{1,0:T(8,128)(2,1)} %v_hbm.1, bf16[2048,4096]{1,0:T(8,128)(2,1)} %w_hbm.1), custom_call_target="tpu_custom_call" | custom-call | tf_op jit(solution)/shard_map/pallas_call | solution.py:422
  47.6 2.1 %copy.8 = bf16[96,4096]{1,0:T(8,128)(2,1)} copy(bf16[96,4096]{1,0:T(8,128)(2,1)} %shard_map.64) | data formatting | bytes 1572864

commit v4 on v3

--- a/solution.py
+++ b/solution.py
@@ -19,16 +19,16 @@
 
 
 def kernel(
-    line, span_ref, doc_ref, q_hbm, k_hbm, v_hbm, w_hbm, out_hbm,
-    kv, kv_out, q_in, q_out, marks, q_t, slot_of, k_near, v_near, raw, held,
+    line, span_hbm, doc_hbm, q_hbm, k_hbm, v_hbm, w_hbm, out_hbm,
+    kv, kv_out, q_in, q_out, marks, q_t, span_ref, doc_ref, slot_of, k_near, v_near, raw, held,
     w_vmem, attn, o_out, partial, outgoing, incoming, kept, ready,
-    load_kv, load_q, w_sem, send_kv, send_q, send_o, send_z, recv_kv, recv_q, recv_o, out_send, out_recv, out_sem, turn,
+    load_kv, load_q, w_sem, send_kv, send_q, send_o, send_z, recv_kv, recv_q, recv_o, out_send, out_recv, out_sem, table_sem, turn,
 ):
     rows = k_hbm.shape[0]
     span_len = rows // 2
     wide = q_hbm.shape[1] // MATES
     group = wide // HEAD_WIDTH
-    slots = span_ref.shape[0]
+    slots = span_hbm.shape[0]
     reach = k_near.shape[1] // span_len
     me = lax.axis_index("cp")
     hd = lax.axis_index("hd")
@@ -109,9 +109,15 @@
         def _():
             z_block(0, 0, 0, src, mate(1)).wait_recv()
 
+    tables = [
+        pltpu.make_async_copy(span_hbm, span_ref, table_sem.at[0]),
+        pltpu.make_async_copy(doc_hbm, doc_ref, table_sem.at[1]),
+    ]
     for i in range(MATES):
         for h in range(2):
             kv_load(i, h).start()
+    for table in tables:
+        table.start()
     for i in range(MATES):
         q_load(i).start()
 
@@ -164,6 +170,8 @@
         send_queries()
 
 
+    for table in tables:
+        table.wait()
     docs = doc_ref[...]
     starts = [jnp.zeros((1, 1), f32)]
     for d in range(1, DOCS):
@@ -422,7 +430,7 @@
     return pl.pallas_call(
         functools.partial(kernel, line),
         out_shape=jax.ShapeDtypeStruct((half, model), bf16),
-        in_specs=[spec(pltpu.SMEM), spec(vmem), spec(hbm), spec(hbm), spec(hbm), spec(hbm)],
+        in_specs=[spec(hbm), spec(hbm), spec(hbm), spec(hbm), spec(hbm), spec(hbm)],
         out_specs=spec(hbm),
         scratch_shapes=[
             vmem((cp, 2, 2, span_len, HEAD_WIDTH), bf16),
@@ -431,6 +439,8 @@
             vmem((MATES, rows, wide), bf16),
             vmem((slots + 1, span_len, HEAD_WIDTH), bf16),
             vmem((2 * MATES, 2 * HEAD_WIDTH, lanes), bf16),
+            pltpu.SMEM((slots,), jnp.int32),
+            vmem((doc_ids.shape[0] // 128, 128), jnp.int32),
             pltpu.SMEM((slots,), jnp.int32),
             vmem((2, near, 2 * HEAD_WIDTH), bf16),
             vmem((3, near, HEAD_WIDTH), bf16),
@@ -445,7 +455,7 @@
             vmem((count, half, width), f32),
             vmem((count, half, width), bf16),
             dma((MATES, 2, 2)), dma((MATES,)), dma((MATES,)), dma((MATES, 2)), dma((MATES,)), dma((MATES, 2)),
-            dma((line, 2, MATES, 2)), dma((cp, 2)), dma((MATES,)), dma((MATES, 2)), dma((count,)), dma((count,)), dma((count,)),
+            dma((line, 2, MATES, 2)), dma((cp, 2)), dma((MATES,)), dma((MATES, 2)), dma((count,)), dma((count,)), dma((count,)), dma((2,)),
             pltpu.SemaphoreType.REGULAR((2,)),
         ],
         compiler_params=pltpu.CompilerParams(

time: 50 us -> 49.3 us (0.986)
  Pallas kernels: 47.6 us -> 47 us
    pallas_call x1, Pallas kernels: 47.6 us -> 47 us  [local(): pl.pallas_call(functools.partial(kernel, line), out_shape=jax.ShapeDtypeS...]
where the time goes in v4:
time: 49.3 us; the launch traced here: 49.1 us
  Pallas kernels  47 us (95%)
  local copies, waits for them, and re-layouts  2.06 us (4%)
    pallas_call x1, Pallas kernels, local(): pl.pallas_call(functools.partial(kernel, line), out_shape=jax.ShapeDtypeS...  47 us
    unnamed x1, local copies, waits for them, and re-layouts  2.06 us

profile of v4, /device:TPU:0, one launch (start us, length us, event | category | flops | bytes accessed | tf_op | source)
XLA Modules:
  0.0 49.1 jit_solution(1697843409247834739)
XLA Ops:
  0.0 47.0 %shard_map.64 = bf16[96,4096]{1,0:T(8,128)(2,1)} custom-call(s32[32]{0:T(128)} %span_hbm.1, s32[24,128]{1,0:T(8,128)} %bitcast.1, bf16[192,2048]{1,0:T(8,128)(2,1)} %q_hbm.1, bf16[192,512]{1,0:T(8,128)(2,1)} %k_hbm.1, bf16[192,512]{1,0:T(8,128)(2,1)} %v_hbm.1, bf16[2048,4096]{1,0:T(8,128)(2,1)} %w_hbm.1), custom_call_target="tpu_custom_call" | custom-call | tf_op jit(solution)/shard_map/pallas_call | solution.py:430
  47.0 2.1 %copy.8 = bf16[96,4096]{1,0:T(8,128)(2,1)} copy(bf16[96,4096]{1,0:T(8,128)(2,1)} %shard_map.64) | data formatting | bytes 1572864
